TPU v7x, 32 devices: a whole 2x2x4 slice. The times are simulated.
32 devices in a mesh: dp: 8 (over y, x, core), tensor: 4 (over z).
Axes of the slice: x: 2, y: 2, z: 4, core: 2. Of those that a mesh axis runs over, the one named last changes fastest.
Arguments:
- images: bfloat16 [32, 320, 1024], P('dp', None, 'tensor'), may hold values from -6 to 6
- lengths: int32 [32], P('dp'), may hold values from 224 to 320, as said below
- cotangent: bfloat16 [32, 320, 1024], P('dp', None, 'tensor'), may hold values from -6 to 6
- norm1_gain: float32 [1024], replicated, may hold values from 0.5 to 1.5
- norm1_shift: float32 [1024], replicated, may hold values from -1.75 to 1.75
- w_qkv: bfloat16 [1024, 3, 1024], P(None, None, 'tensor'), may hold values from -0.1875 to 0.1875
- qv_bias: float32 [2, 1024], P(None, 'tensor'), may hold values from -3 to 3
- w_proj: bfloat16 [1024, 1024], P('tensor'), may hold values from -1.5 to 1.5
- proj_bias: float32 [1024], replicated, may hold values from -3 to 3
- norm2_gain: float32 [1024], replicated, may hold values from 0.5 to 1.5
- norm2_shift: float32 [1024], replicated, may hold values from -1.75 to 1.75
- w_fc1: bfloat16 [1024, 4096], P(None, 'tensor'), may hold values from -0.1875 to 0.1875
- fc1_bias: float32 [4096], P('tensor'), may hold values from -3 to 3
- w_fc2: bfloat16 [4096, 1024], P('tensor'), may hold values from -0.09375 to 0.09375
- fc2_bias: float32 [1024], replicated, may hold values from -3 to 3
Outputs:
- output: bfloat16 [32, 320, 1024], P('dp', None, 'tensor')
- input_grad: bfloat16 [32, 320, 1024], P('dp', None, 'tensor')
- grad_norm1_gain: float32 [1024], replicated
- grad_norm1_shift: float32 [1024], replicated
- grad_w_qkv: float32 [1024, 3, 1024], P(None, None, 'tensor')
- grad_qv_bias: float32 [2, 1024], P(None, 'tensor')
- grad_w_proj: float32 [1024, 1024], P('tensor')
- grad_proj_bias: float32 [1024], replicated
- grad_norm2_gain: float32 [1024], replicated
- grad_norm2_shift: float32 [1024], replicated
- grad_w_fc1: float32 [1024, 4096], P(None, 'tensor')
- grad_fc1_bias: float32 [4096], P('tensor')
- grad_w_fc2: float32 [4096, 1024], P('tensor')
- grad_fc2_bias: float32 [1024], replicated
Inputs may be any that keep to these rules, and one draw needn't show every extreme that they name: lengths[i] is the number of valid slots of image i, which come first; some image has all 320 slots valid in every draw.
All inputs are finite; a program needn't handle non-finite values.
Results may differ from a plain program's by a relative error of at most 0.02.
Values may be sent and summed in bfloat16 or wider, within the bound.
A program may use at most 192 MiB of HBM per device.

v0:
```python
import jax
import jax.numpy as jnp
from jax import lax
from jax.sharding import PartitionSpec as P

HEAD_DIM = 64
EPS = 1e-06
MASKED = -1e30


def norm_rows(values, gain_row, shift_row):
    row_mean = jnp.mean(values, axis=-1, keepdims=True)
    centered = values - row_mean
    spread = jnp.mean(centered * centered, axis=-1, keepdims=True)
    inverse = lax.rsqrt(spread + EPS)
    unit_rows = centered * inverse
    return (unit_rows * gain_row + shift_row, unit_rows, inverse)


def norm_back(gradient, unit_rows, inverse, gain_row):
    scaled = gradient * gain_row
    first_mean = jnp.mean(scaled, axis=-1, keepdims=True)
    cross_mean = jnp.mean(scaled * unit_rows, axis=-1, keepdims=True)
    return inverse * (scaled - first_mean - unit_rows * cross_mean)


def scores_of(queries, key_heads, key_mask, score_scale):
    raw_scores = (
        jnp.einsum("bqhe,bkhe->bhqk", queries, key_heads, preferred_element_type=jnp.float32)
        * score_scale
    )
    return jnp.where(key_mask, raw_scores, MASKED)


def exact_gelu(values):
    return jax.nn.gelu(values, approximate=False)


def swap_with(values, axis, size, stride):
    return lax.ppermute(values, axis, [(i, i ^ stride) for i in range(size)])


def halving_sum(blocks, axis, size):
    me = lax.axis_index(axis)
    steps = size.bit_length() - 1
    assert 1 << steps == size
    held = [block.astype(jnp.float32) for block in blocks]
    for step in range(steps):
        bit = me >> step & 1
        kept, given = ([], [])
        for block in held:
            half = block.shape[0] // 2
            kept.append(lax.dynamic_slice_in_dim(block, bit * half, half, 0))
            given.append(
                lax.dynamic_slice_in_dim(block, (1 - bit) * half, half, 0).astype(jnp.bfloat16)
            )
        got = swap_with(tuple(given), axis, size, 1 << step)
        held = [mine + theirs.astype(jnp.float32) for mine, theirs in zip(kept, got)]
    held = [block.astype(jnp.bfloat16) for block in held]
    for step in reversed(range(steps)):
        bit = me >> step & 1
        got = swap_with(tuple(held), axis, size, 1 << step)
        held = [
            jnp.where(bit == 0, jnp.concatenate([mine, theirs]), jnp.concatenate([theirs, mine]))
            for mine, theirs in zip(held, got)
        ]
    return [block.astype(jnp.float32) for block in held]


def doubling_sum(values, axis, size):
    steps = size.bit_length() - 1
    assert 1 << steps == size
    values = [value.astype(jnp.bfloat16) for value in values]
    for step in range(steps):
        got = swap_with(tuple(values), axis, size, 1 << step)
        values = [
            (mine.astype(jnp.float32) + theirs.astype(jnp.float32)).astype(jnp.bfloat16)
            for mine, theirs in zip(values, got)
        ]
    return [value.astype(jnp.float32) for value in values]


def per_device(
    images,
    lengths,
    cotangent,
    norm1_gain,
    norm1_shift,
    w_qkv,
    qv_bias,
    w_proj,
    proj_bias,
    norm2_gain,
    norm2_shift,
    w_fc1,
    fc1_bias,
    w_fc2,
    fc2_bias,
):
    images_here, slot_count, col_count = images.shape
    model_width = w_qkv.shape[0]
    local_width = w_qkv.shape[2]
    heads_here = local_width // HEAD_DIM
    row_count = images_here * slot_count
    score_scale = HEAD_DIM ** (-0.5)
    first_col = lax.axis_index("tensor") * col_count
    full_images, full_cot = (
        lax.all_gather(images, "tensor", axis=2, tiled=True),
        lax.all_gather(cotangent, "tensor", axis=2, tiled=True),
    )
    slot_ids = jnp.arange(slot_count, dtype=jnp.int32)
    valid_slots = (slot_ids[None, :] < lengths[:, None]).astype(jnp.float32)
    keep_rows = valid_slots.reshape(row_count, 1)
    row_values = full_images.reshape(row_count, model_width).astype(jnp.float32) * keep_rows
    normed1, unit1, inverse1 = norm_rows(row_values, norm1_gain, norm1_shift)
    normed1 = normed1.astype(jnp.bfloat16)
    qkv_bias = jnp.concatenate([qv_bias[0], jnp.zeros_like(qv_bias[0]), qv_bias[1]])
    w_flat = w_qkv.reshape(model_width, 3 * local_width)
    qkv_rows = (jnp.dot(normed1, w_flat, preferred_element_type=jnp.float32) + qkv_bias).astype(
        jnp.bfloat16
    )
    qkv_rows = qkv_rows.reshape(images_here, slot_count, 3, heads_here, HEAD_DIM)
    queries = qkv_rows[:, :, 0]
    key_heads = qkv_rows[:, :, 1]
    value_heads = qkv_rows[:, :, 2]
    key_mask = valid_slots[:, None, None, :] > 0
    scores = scores_of(queries, key_heads, key_mask, score_scale)
    row_top = jnp.max(scores, axis=-1, keepdims=True)
    shifted = jnp.exp(scores - row_top)
    row_total = jnp.sum(shifted, axis=-1, keepdims=True)
    probability = (shifted / row_total).astype(jnp.bfloat16)
    log_total = row_top + jnp.log(row_total)
    mixed = jnp.einsum(
        "bhqk,bkhe->bqhe", probability, value_heads, preferred_element_type=jnp.float32
    ).astype(jnp.bfloat16)
    mixed_rows = mixed.reshape(row_count, local_width)
    attn_part = jnp.dot(mixed_rows, w_proj, preferred_element_type=jnp.float32)
    middle = (
        row_values
        + lax.psum(attn_part.astype(jnp.bfloat16), "tensor").astype(jnp.float32)
        + proj_bias
    )
    normed2, unit2, inverse2 = norm_rows(middle, norm2_gain, norm2_shift)
    normed2 = normed2.astype(jnp.bfloat16)
    pre_act = jnp.dot(normed2, w_fc1, preferred_element_type=jnp.float32) + fc1_bias
    activated = exact_gelu(pre_act).astype(jnp.bfloat16)
    ff_part = jnp.dot(activated, w_fc2, preferred_element_type=jnp.float32).astype(jnp.bfloat16)
    grad_out = full_cot.reshape(row_count, model_width).astype(jnp.float32) * keep_rows
    grad_ff = grad_out.astype(jnp.bfloat16)
    grad_fc2_bias = jnp.sum(grad_ff, axis=0, dtype=jnp.float32)
    grad_w_fc2 = jnp.einsum("rf,rd->fd", activated, grad_ff, preferred_element_type=jnp.float32)
    grad_act = jnp.einsum("rd,fd->rf", grad_ff, w_fc2, preferred_element_type=jnp.float32)
    gelu_pull = jax.vjp(exact_gelu, pre_act)[1]
    grad_pre = gelu_pull(grad_act)[0].astype(jnp.bfloat16)
    grad_fc1_bias = jnp.sum(grad_pre, axis=0, dtype=jnp.float32)
    grad_w_fc1 = jnp.einsum("rd,rf->df", normed2, grad_pre, preferred_element_type=jnp.float32)
    hidden_part = jnp.einsum("rf,df->rd", grad_pre, w_fc1, preferred_element_type=jnp.float32)
    grad_normed2 = lax.psum(hidden_part.astype(jnp.bfloat16), "tensor").astype(jnp.float32)
    ff_part, grad_normed2 = lax.optimization_barrier((ff_part, grad_normed2))
    ff_share = lax.psum_scatter(ff_part, "tensor", scatter_dimension=1, tiled=True).astype(
        jnp.float32
    )
    middle_cols = lax.dynamic_slice_in_dim(middle, first_col, col_count, 1)
    bias_cols = lax.dynamic_slice_in_dim(fc2_bias, first_col, col_count, 0)
    output = ((middle_cols + ff_share + bias_cols) * keep_rows).astype(jnp.bfloat16)
    output = output.reshape(images_here, slot_count, col_count)
    dp_size = lax.axis_size("dp")
    tensor_size = lax.axis_size("tensor")
    grad_norm2_gain = jnp.sum(grad_normed2 * unit2, axis=0)
    grad_norm2_shift = jnp.sum(grad_normed2, axis=0)
    grad_middle = grad_out + norm_back(grad_normed2, unit2, inverse2, norm2_gain)
    grad_attn = grad_middle.astype(jnp.bfloat16)
    grad_proj_bias = jnp.sum(grad_attn, axis=0, dtype=jnp.float32)
    grad_w_proj = jnp.einsum("rc,rd->cd", mixed_rows, grad_attn, preferred_element_type=jnp.float32)
    grad_w_fc1, grad_w_fc2, grad_w_proj = halving_sum(
        [grad_w_fc1, grad_w_fc2, grad_w_proj], "dp", dp_size
    )
    grad_fc1_bias, grad_fc2_bias, grad_proj_bias, grad_norm2_gain, grad_norm2_shift = doubling_sum(
        [grad_fc1_bias, grad_fc2_bias, grad_proj_bias, grad_norm2_gain, grad_norm2_shift],
        "dp",
        dp_size,
    )
    grad_mixed = jnp.einsum(
        "rd,cd->rc", grad_attn, w_proj, preferred_element_type=jnp.float32
    ).astype(jnp.bfloat16)
    grad_mixed = grad_mixed.reshape(images_here, slot_count, heads_here, HEAD_DIM)
    scores_again = scores_of(queries, key_heads, key_mask, score_scale)
    weights_soft = jnp.exp(scores_again - log_total)
    grad_value = jnp.einsum(
        "bhqk,bqhe->bkhe",
        weights_soft.astype(jnp.bfloat16),
        grad_mixed,
        preferred_element_type=jnp.float32,
    )
    grad_prob = jnp.einsum(
        "bqhe,bkhe->bhqk", grad_mixed, value_heads, preferred_element_type=jnp.float32
    )
    row_dot = jnp.sum(weights_soft * grad_prob, axis=-1, keepdims=True)
    grad_scores = (weights_soft * (grad_prob - row_dot)).astype(jnp.bfloat16)
    grad_query = (
        jnp.einsum("bhqk,bkhe->bqhe", grad_scores, key_heads, preferred_element_type=jnp.float32)
        * score_scale
    )
    grad_key = (
        jnp.einsum("bhqk,bqhe->bkhe", grad_scores, queries, preferred_element_type=jnp.float32)
        * score_scale
    )
    grad_qkv = jnp.stack([grad_query, grad_key, grad_value], axis=2).astype(jnp.bfloat16)
    grad_qkv = grad_qkv.reshape(row_count, 3 * local_width)
    bias_sums = jnp.sum(grad_qkv, axis=0, dtype=jnp.float32).reshape(3, local_width)
    grad_qv_bias = jnp.stack([bias_sums[0], bias_sums[2]])
    grad_w_qkv = jnp.einsum("rd,rc->dc", normed1, grad_qkv, preferred_element_type=jnp.float32)
    (grad_w_qkv,) = halving_sum([grad_w_qkv], "dp", dp_size)
    grad_w_qkv = grad_w_qkv.reshape(model_width, 3, local_width)
    normed_part = jnp.einsum(
        "rc,dc->rd", grad_qkv, w_flat, preferred_element_type=jnp.float32
    ).astype(jnp.bfloat16)
    output, normed_part = lax.optimization_barrier((output, normed_part))
    grad_normed1 = lax.psum_scatter(normed_part, "tensor", scatter_dimension=1, tiled=True).astype(
        jnp.float32
    )
    term = normed_part.astype(jnp.float32)
    term_gain = term * norm1_gain
    first_stat = jnp.sum(term_gain, axis=1)
    second_stat = jnp.sum(term_gain * unit1, axis=1)
    norm1_terms = jnp.stack([jnp.sum(term * unit1, axis=0), jnp.sum(term, axis=0)])
    first_stat, second_stat, norm1_terms = doubling_sum(
        [first_stat, second_stat, norm1_terms], "tensor", tensor_size
    )
    norm1_sums, grad_qv_bias = doubling_sum([norm1_terms, grad_qv_bias], "dp", dp_size)
    first_mean = first_stat / model_width
    second_mean = second_stat / model_width
    unit1_cols = lax.dynamic_slice_in_dim(unit1, first_col, col_count, 1)
    gain1_cols = lax.dynamic_slice_in_dim(norm1_gain, first_col, col_count, 0)
    input_part = inverse1 * (
        grad_normed1 * gain1_cols - first_mean[:, None] - unit1_cols * second_mean[:, None]
    )
    middle_grad_cols = lax.dynamic_slice_in_dim(grad_middle, first_col, col_count, 1)
    grad_input = (middle_grad_cols + input_part) * keep_rows
    input_grad = grad_input.astype(jnp.bfloat16).reshape(images_here, slot_count, col_count)
    return (
        output,
        input_grad,
        norm1_sums[0],
        norm1_sums[1],
        grad_w_qkv,
        grad_qv_bias,
        grad_w_proj,
        grad_proj_bias,
        grad_norm2_gain,
        grad_norm2_shift,
        grad_w_fc1,
        grad_fc1_bias,
        grad_w_fc2,
        grad_fc2_bias,
    )


def solution(mesh):
    in_specs = (
        P("dp", None, "tensor"),
        P("dp"),
        P("dp", None, "tensor"),
        P(),
        P(),
        P(None, None, "tensor"),
        P(None, "tensor"),
        P("tensor", None),
        P(),
        P(),
        P(),
        P(None, "tensor"),
        P("tensor"),
        P("tensor", None),
        P(),
    )
    out_specs = (
        P("dp", None, "tensor"),
        P("dp", None, "tensor"),
        P(),
        P(),
        P(None, None, "tensor"),
        P(None, "tensor"),
        P("tensor", None),
        P(),
        P(),
        P(),
        P(None, "tensor"),
        P("tensor"),
        P("tensor", None),
        P(),
    )
    return jax.shard_map(
        per_device, mesh=mesh, in_specs=in_specs, out_specs=out_specs, check_vma=False
    )
```

profile of v0, /device:TPU:0, one launch (start us, length us, event | category | flops | bytes accessed | tf_op | source)
XLA Modules:
  0.0 557.9 jit_solution(11959580105190340628)
XLA Ops:
  12.8 54.3 %all-gather.3.cloned.1.call-done = bf16[4,320,1024]{2,1,0:T(8,128)(2,1)} async-done(((bf16[4,320,256]{2,1,0:T(8,128)(2,1)}), bf16[4,320,1024]{2,1,0:T(8,128)(2,1)}) %all-gather.3.cloned.1.call-update) | async-done | bytes 2621456 | tf_op jit(solution)/shard_map/all_gather | solution.py:108
  78.9 6.7 %reshape.273 = bf16[4,320,3,4,64]{4,3,2,1,0:T(4,128)(2,1)} reshape(bf16[1280,768]{1,0:T(8,128)(2,1)} %add_convert_fusion.3) | data formatting | bytes 3932160 | tf_op jit(solution)/shard_map/reshape | solution.py:122
  85.6 3.9 fusion.64
  112.3 9.4 %all-gather.5.cloned.1.call-done = bf16[4,320,1024]{2,1,0:T(8,128)(2,1)} async-done(((bf16[4,320,256]{2,1,0:T(8,128)(2,1)}), bf16[4,320,1024]{2,1,0:T(8,128)(2,1)}) %all-gather.5.cloned.1.call-update) | async-done | bytes 2621456 | tf_op jit(solution)/shard_map/all_gather | solution.py:109
  136.9 90.1 %all-reduce.3.cloned.1.call-done = bf16[1280,1024]{1,0:T(8,128)(2,1)} async-done(((bf16[1280,1024]{1,0:T(8,128)(2,1)}), bf16[1280,1024]{1,0:T(8,128)(2,1)}) %all-reduce.3.cloned.1.call-update) | async-done | bytes 2621456 | tf_op jit(solution)/shard_map/psum | solution.py:140
  227.0 5.0 fusion.63
  238.3 16.9 %fusion.60 = (bf16[1024]{0:T(1024)(128)(2,1)}, bf16[1280,1024]{1,0:T(8,128)(2,1)}, f32[1280,1024]{1,0:T(8,128)S(1)}) fusion(f32[1280,1024]{1,0:T(8,128)S(1)} %fusion.59, f32[1024]{0:T(1024)S(1)} %copy-done.42, bf16[1280,1024]{1,0:T(8,128)(2,1)S(1)} %get-tuple-element.44, bf16[1024,1024]{1,0:T(8,128)(2,1)S(1)} %copy-done), kind=kOutput, calls=%fused_computation.180 | convolution fusion | flops 2781346816 | bytes 17831936 | tf_op jit(solution)/shard_map/rd,fd->rf/dot_general | solution.py:152
  260.9 5.2 fusion.58
  266.1 4.2 convolution_convert_fusion.2
  273.6 6.3 %convolution_convert_fusion.3 = bf16[1280,1024]{1,0:T(8,128)(2,1)} fusion(bf16[1280,1024]{1,0:T(8,128)(2,1)} %copy-done.13, bf16[1024,1024]{1,0:T(8,128)(2,1)S(1)} %copy-done), kind=kOutput, calls=%fused_computation.56 | convolution fusion | flops 2685665280 | bytes 7340032 | tf_op jit(solution)/shard_map/dot_general | solution.py:147
  288.3 9.0 %collective-permute-done.43 = bf16[256,1024]{1,0:T(8,128)(2,1)S(1)} collective-permute-done((bf16[256,1024]{1,0:T(8,128)(2,1)S(1)}, bf16[256,1024]{1,0:T(8,128)(2,1)S(1)}, u32[]{:S(2)}, u32[]{:S(2)}) %collective-permute-start.43) | collective-permute-done | bytes 524320 | tf_op jit(solution)/shard_map/ppermute | solution.py:40
  298.8 9.4 %collective-permute-done.34 = bf16[256,1024]{1,0:T(8,128)(2,1)S(1)} collective-permute-done((bf16[256,1024]{1,0:T(8,128)(2,1)S(1)}, bf16[256,1024]{1,0:T(8,128)(2,1)S(1)}, u32[]{:S(2)}, u32[]{:S(2)}) %collective-permute-start.34) | collective-permute-done | bytes 524320 | tf_op jit(solution)/shard_map/ppermute | solution.py:40
  311.9 5.7 %collective-permute-done.35 = bf16[128,1024]{1,0:T(8,128)(2,1)S(1)} collective-permute-done((bf16[128,1024]{1,0:T(8,128)(2,1)S(1)}, bf16[128,1024]{1,0:T(8,128)(2,1)S(1)}, u32[]{:S(2)}, u32[]{:S(2)}) %collective-permute-start.35) | collective-permute-done | bytes 262176 | tf_op jit(solution)/shard_map/ppermute | solution.py:40
  329.9 44.2 %all-reduce.5.cloned.1.call-done = bf16[1280,1024]{1,0:T(8,128)(2,1)} async-done(((bf16[1280,1024]{1,0:T(8,128)(2,1)}), bf16[1280,1024]{1,0:T(8,128)(2,1)}) %all-reduce.5.cloned.1.call-update) | async-done | bytes 2621456 | tf_op jit(solution)/shard_map/psum | solution.py:158
  376.7 5.3 multiply_reduce_fusion.1
  393.4 6.4 %fusion.29 = bf16[4,320,1,4,64]{1,4,3,0,2:T(8,128)(2,1)} fusion(bf16[4,320,4,64]{1,3,2,0:T(8,128)(2,1)} %copy.54, f32[4,4,320]{2,1,0:T(4,128)} %bitcast.109, f32[4,4,320,320]{2,3,1,0:T(8,128)} %copy-done.1, pred[4,320]{1,0:T(4,128)(4,1)S(1)} %copy-done.34), kind=kOutput, calls=%fused_computation.80 | convolution fusion | flops 216596480 | bytes 7886080 | tf_op jit(solution)/shard_map/bhqk,bqhe->bkhe/dot_general | solution.py:189
  399.8 5.4 multiply_reduce_fusion
  416.1 5.3 copy.59
  421.5 4.7 convert_element_type.555
  428.0 4.7 fusion.69
  435.3 3.8 convolution_convert_fusion
  504.9 4.4 fusion.22
  509.4 5.3 fusion.21
  522.0 6.8 %fusion.5 = (bf16[1024]{0:T(1024)(128)(2,1)S(1)}, bf16[1280]{0:T(1024)(128)(2,1)S(1)}, bf16[1280]{0:T(1024)(128)(2,1)S(1)}, f32[1280,1024]{1,0:T(8,128)}) fusion(bf16[1280,1024]{1,0:T(8,128)(2,1)} %convolution_convert_fusion, f32[1280]{0:T(1024)S(1)} %copy-done.31, f32[1280]{0:T(1024)} %div.43, f32[1280]{0:T(1024)S(1)} %reshape.271, ...), kind=kLoop, calls=%fused_computation.14 | loop fusion | flops 14414336 | bytes 10512384 | tf_op jit(solution)/shard_map/reduce_sum | solution.py:226
  (343 shorter events, 219.9 us)
Async XLA Ops:
  7.2 60.0 %all-gather.3.cloned.1.call-start = ((), (), s32[]{:S(2)}) async-start(), calls=%async_computation.2 | async-start | bytes 3276800 | tf_op jit(solution)/shard_map/all_gather | solution.py:108
  8.0 113.8 %all-gather.5.cloned.1.call-start = ((), (), s32[]{:S(2)}) async-start(), calls=%async_computation.4 | async-start | bytes 3276800 | tf_op jit(solution)/shard_map/all_gather | solution.py:109
  8.7 218.3 %all-reduce.3.cloned.1.call-start = ((), (), s32[]{:S(2)}) async-start(), calls=%async_computation.3 | async-start | bytes 5242880 | tf_op jit(solution)/shard_map/psum | solution.py:140
  112.3 261.8 %all-reduce.5.cloned.1.call-start = ((), (), s32[]{:S(2)}) async-start(), calls=%async_computation.5 | async-start | bytes 5242880 | tf_op jit(solution)/shard_map/psum | solution.py:158
  260.9 19.0 %collective-permute-start.42 = (bf16[512,1024]{1,0:T(8,128)(2,1)}, bf16[512,1024]{1,0:T(8,128)(2,1)}, u32[]{:S(2)}, u32[]{:S(2)}) collective-permute-start(bf16[512,1024]{1,0:T(8,128)(2,1)} %dynamic-slice_convert_fusion), channel_id=1, source_target_pairs={{0,4},{4,0},{8,12},{12,8},{16,20},{20,16},{24,28},{28,24},{1,5},{5... | collective-permute-start | bytes 3145736 | tf_op jit(solution)/shard_map/ppermute | solution.py:40
  270.3 16.0 %collective-permute-start.39 = (bf16[1024]{0:T(1024)(128)(2,1)}, bf16[1024]{0:T(1024)(128)(2,1)}, u32[]{:S(2)}, u32[]{:S(2)}) collective-permute-start(bf16[1024]{0:T(1024)(128)(2,1)} %get-tuple-element.29), channel_id=1, source_target_pairs={{0,4},{4,0},{8,12},{12,8},{16,20},{20,16},{24,28},{28,24},{1,5},{5... | collective-permute-start | bytes 6152 | tf_op jit(solution)/shard_map/ppermute | solution.py:40
  270.8 207.2 %reduce-scatter.3.cloned.1.call-start = ((), (), s32[]{:S(2)}) async-start(), calls=%async_computation.6 | async-start | bytes 3276800 | tf_op jit(solution)/shard_map/reduce_scatter | solution.py:160
  282.4 14.9 %collective-permute-start.43 = (bf16[256,1024]{1,0:T(8,128)(2,1)S(1)}, bf16[256,1024]{1,0:T(8,128)(2,1)S(1)}, u32[]{:S(2)}, u32[]{:S(2)}) collective-permute-start(bf16[256,1024]{1,0:T(8,128)(2,1)S(1)} %dynamic-slice_convert_fusion.3), channel_id=1, source_target_pairs={{0,8},{4,12},{8,0},{12,4},{16,24},{20,28},{24,16},{28,20},{1,9},{5... | collective-permute-start | bytes 1572872 | tf_op jit(solution)/shard_map/ppermute | solution.py:40
  285.5 22.6 %collective-permute-start.34 = (bf16[256,1024]{1,0:T(8,128)(2,1)S(1)}, bf16[256,1024]{1,0:T(8,128)(2,1)S(1)}, u32[]{:S(2)}, u32[]{:S(2)}) collective-permute-start(bf16[256,1024]{1,0:T(8,128)(2,1)S(1)} %dynamic-slice_convert_fusion.4), channel_id=1, source_target_pairs={{0,8},{4,12},{8,0},{12,4},{16,24},{20,28},{24,16},{28,20},{1,9},{5... | collective-permute-start | bytes 1572872 | tf_op jit(solution)/shard_map/ppermute | solution.py:40
  287.1 22.7 %collective-permute-start.40 = (bf16[1024]{0:T(1024)(128)(2,1)S(1)}, bf16[1024]{0:T(1024)(128)(2,1)S(1)}, u32[]{:S(2)}, u32[]{:S(2)}) collective-permute-start(bf16[1024]{0:T(1024)(128)(2,1)S(1)} %add_convert_fusion.22), channel_id=1, source_target_pairs={{0,8},{4,12},{8,0},{12,4},{16,24},{20,28},{24,16},{28,20},{1,9},{5... | collective-permute-start | bytes 6152 | tf_op jit(solution)/shard_map/ppermute | solution.py:40
  297.5 13.1 %collective-permute-start.44 = (bf16[128,1024]{1,0:T(8,128)(2,1)S(1)}, bf16[128,1024]{1,0:T(8,128)(2,1)S(1)}, u32[]{:S(2)}, u32[]{:S(2)}) collective-permute-start(bf16[128,1024]{1,0:T(8,128)(2,1)S(1)} %dynamic-slice_convert_fusion.6), channel_id=1, source_target_pairs={{0,16},{4,20},{8,24},{12,28},{16,0},{20,4},{24,8},{28,12},{1,17},{... | collective-permute-start | bytes 786440 | tf_op jit(solution)/shard_map/ppermute | solution.py:40
  324.2 114.9 %collective-permute-start.46 = (bf16[256,1024]{1,0:T(8,128)(2,1)}, bf16[256,1024]{1,0:T(8,128)(2,1)}, u32[]{:S(2)}, u32[]{:S(2)}) collective-permute-start(bf16[256,1024]{1,0:T(8,128)(2,1)} %maximum_select_fusion.9), channel_id=1, source_target_pairs={{0,8},{4,12},{8,0},{12,4},{16,24},{20,28},{24,16},{28,20},{1,9},{5... | collective-permute-start | bytes 1572872 | tf_op jit(solution)/shard_map/ppermute | solution.py:40
  328.7 113.0 %collective-permute-start.37 = (bf16[256,1024]{1,0:T(8,128)(2,1)}, bf16[256,1024]{1,0:T(8,128)(2,1)}, u32[]{:S(2)}, u32[]{:S(2)}) collective-permute-start(bf16[256,1024]{1,0:T(8,128)(2,1)} %maximum_select_fusion.8), channel_id=1, source_target_pairs={{0,8},{4,12},{8,0},{12,4},{16,24},{20,28},{24,16},{28,20},{1,9},{5... | collective-permute-start | bytes 1572872 | tf_op jit(solution)/shard_map/ppermute | solution.py:40
  412.0 135.5 %reduce-scatter.5.cloned.1.call-start = ((), (), s32[]{:S(2)}) async-start(), calls=%async_computation.7 | async-start | bytes 3276800 | tf_op jit(solution)/shard_map/reduce_scatter | solution.py:219
  412.0 33.4 %collective-permute-start.24 = (bf16[1024]{0:T(1024)(128)(2,1)S(1)}, bf16[1024]{0:T(1024)(128)(2,1)S(1)}, u32[]{:S(2)}, u32[]{:S(2)}) collective-permute-start(bf16[1024]{0:T(1024)(128)(2,1)S(1)} %copy-done.40), channel_id=1, source_target_pairs={{0,4},{4,0},{8,12},{12,8},{16,20},{20,16},{24,28},{28,24},{1,5},{5... | collective-permute-start | bytes 6152 | tf_op jit(solution)/shard_map/ppermute | solution.py:40
  412.1 33.4 %collective-permute-start.27 = (bf16[1024]{0:T(1024)(128)(2,1)S(1)}, bf16[1024]{0:T(1024)(128)(2,1)S(1)}, u32[]{:S(2)}, u32[]{:S(2)}) collective-permute-start(bf16[1024]{0:T(1024)(128)(2,1)S(1)} %copy-done.39), channel_id=1, source_target_pairs={{0,4},{4,0},{8,12},{12,8},{16,20},{20,16},{24,28},{28,24},{1,5},{5... | collective-permute-start | bytes 6152 | tf_op jit(solution)/shard_map/ppermute | solution.py:40
  412.6 36.6 %collective-permute-start.30 = (bf16[1024]{0:T(1024)(128)(2,1)S(1)}, bf16[1024]{0:T(1024)(128)(2,1)S(1)}, u32[]{:S(2)}, u32[]{:S(2)}) collective-permute-start(bf16[1024]{0:T(1024)(128)(2,1)S(1)} %copy-done.38), channel_id=1, source_target_pairs={{0,4},{4,0},{8,12},{12,8},{16,20},{20,16},{24,28},{28,24},{1,5},{5... | collective-permute-start | bytes 6152 | tf_op jit(solution)/shard_map/ppermute | solution.py:40
  439.2 18.9 %collective-permute-start.18 = (bf16[128,1024]{1,0:T(8,128)(2,1)}, bf16[128,1024]{1,0:T(8,128)(2,1)S(1)}, u32[]{:S(2)}, u32[]{:S(2)}) collective-permute-start(bf16[128,1024]{1,0:T(8,128)(2,1)} %dynamic-slice_convert_fusion.8), channel_id=1, source_target_pairs={{0,4},{4,0},{8,12},{12,8},{16,20},{20,16},{24,28},{28,24},{1,5},{5... | collective-permute-start | bytes 786440 | tf_op jit(solution)/shard_map/ppermute | solution.py:40
  445.0 21.7 %collective-permute-start.9 = (bf16[512,768]{0,1:T(8,128)(2,1)}, bf16[512,768]{0,1:T(8,128)(2,1)S(1)}, u32[]{:S(2)}, u32[]{:S(2)}) collective-permute-start(bf16[512,768]{0,1:T(8,128)(2,1)} %dynamic-slice_convert_fusion.2), channel_id=1, source_target_pairs={{0,4},{4,0},{8,12},{12,8},{16,20},{20,16},{24,28},{28,24},{1,5},{5... | collective-permute-start | bytes 2359304 | tf_op jit(solution)/shard_map/ppermute | solution.py:40
  445.4 59.5 %collective-permute-start.47 = (bf16[512,1024]{1,0:T(8,128)(2,1)S(1)}, bf16[512,1024]{1,0:T(8,128)(2,1)}, u32[]{:S(2)}, u32[]{:S(2)}) collective-permute-start(bf16[512,1024]{1,0:T(8,128)(2,1)S(1)} %maximum_select_fusion.4), channel_id=1, source_target_pairs={{0,4},{4,0},{8,12},{12,8},{16,20},{20,16},{24,28},{28,24},{1,5},{5... | collective-permute-start | bytes 3145736 | tf_op jit(solution)/shard_map/ppermute | solution.py:40
  449.2 60.2 %collective-permute-start.38 = (bf16[512,1024]{1,0:T(8,128)(2,1)}, bf16[512,1024]{1,0:T(8,128)(2,1)}, u32[]{:S(2)}, u32[]{:S(2)}) collective-permute-start(bf16[512,1024]{1,0:T(8,128)(2,1)} %maximum_select_fusion.3), channel_id=1, source_target_pairs={{0,4},{4,0},{8,12},{12,8},{16,20},{20,16},{24,28},{28,24},{1,5},{5... | collective-permute-start | bytes 3145736 | tf_op jit(solution)/shard_map/ppermute | solution.py:40
  465.0 21.7 %collective-permute-start.26 = (bf16[1024]{0:T(1024)(128)(2,1)S(1)}, bf16[1024]{0:T(1024)(128)(2,1)}, u32[]{:S(2)}, u32[]{:S(2)}) collective-permute-start(bf16[1024]{0:T(1024)(128)(2,1)S(1)} %add_convert_fusion.30), channel_id=1, source_target_pairs={{0,16},{4,20},{8,24},{12,28},{16,0},{20,4},{24,8},{28,12},{1,17},{... | collective-permute-start | bytes 6152 | tf_op jit(solution)/shard_map/ppermute | solution.py:40
  471.0 23.2 %collective-permute-start.29 = (bf16[1024]{0:T(1024)(128)(2,1)S(1)}, bf16[1024]{0:T(1024)(128)(2,1)}, u32[]{:S(2)}, u32[]{:S(2)}) collective-permute-start(bf16[1024]{0:T(1024)(128)(2,1)S(1)} %add_convert_fusion.27), channel_id=1, source_target_pairs={{0,16},{4,20},{8,24},{12,28},{16,0},{20,4},{24,8},{28,12},{1,17},{... | collective-permute-start | bytes 6152 | tf_op jit(solution)/shard_map/ppermute | solution.py:40
  503.8 13.6 %collective-permute-start.14 = (bf16[512,768]{0,1:T(8,128)(2,1)}, bf16[512,768]{0,1:T(8,128)(2,1)}, u32[]{:S(2)}, u32[]{:S(2)}) collective-permute-start(bf16[512,768]{0,1:T(8,128)(2,1)} %maximum_select_fusion.6), channel_id=1, source_target_pairs={{0,4},{4,0},{8,12},{12,8},{16,20},{20,16},{24,28},{28,24},{1,5},{5... | collective-permute-start | bytes 2359304 | tf_op jit(solution)/shard_map/ppermute | solution.py:40
  (86 other events, 948.5 us)
Sparse Core Ops, SparseCore 0:
  9.6 57.5 all-gather.2
  68.7 52.9 all-gather.4
  124.7 102.2 all-reduce.2
  271.0 103.0 all-reduce.4
  412.1 51.3 reduce-scatter.2
  480.8 50.0 reduce-scatter.4
where the time goes:
time: 568 us; the launch traced here: 558 us
  waiting for transfers between devices  261 us (46%)
  other arithmetic  92.1 us (16%)
  matrix products  78.6 us (14%)
  local copies, waits for them, and re-layouts  64.3 us (11%)
  starting transfers between devices  46.3 us (8%)
  between operations  15.6 us (3%)
    psum x1, waiting for transfers between devices, per_device(): lax.psum(attn_part.astype(jnp.bfloat16), 'tensor').astype(jnp.float32)  90.1 us
    ppermute x51, waiting for transfers between devices, swap_with(): return lax.ppermute(values, axis, [(i, i ^ stride) for i in range(size)])  61.5 us
    all_gather x1, waiting for transfers between devices, per_device(): lax.all_gather(images, 'tensor', axis=2, tiled=True)  54.3 us
    ppermute x51, starting transfers between devices, swap_with(): return lax.ppermute(values, axis, [(i, i ^ stride) for i in range(size)])  46.1 us
    psum x1, waiting for transfers between devices, per_device(): lax.psum(hidden_part.astype(jnp.bfloat16), 'tensor').astype(jnp.float32)  44.2 us
    unnamed x110, local copies, waits for them, and re-layouts  18.4 us
    dot_general x1, matrix products, per_device(): jnp.einsum('rd,fd->rf', grad_ff, w_fc2, preferred_element_type=jnp.float32)  16.9 us
    convert_element_type x4, other arithmetic, halving_sum(): return [block.astype(jnp.float32) for block in held]  12.9 us
  transfers between devices with their start and end apart: 57, of which 24 were waited for; matrix products, arithmetic and copies ran while one was open for 35% of the time, Pallas kernels for 0%

commit v1 on v0

--- a/solution.py
+++ b/solution.py
@@ -2,6 +2,7 @@
 import jax.numpy as jnp
 from jax import lax
 from jax.sharding import PartitionSpec as P
+from jax.lax import axis_index, axis_size, ppermute
 
 HEAD_DIM = 64
 EPS = 1e-06
@@ -104,8 +105,36 @@
     row_count = images_here * slot_count
     score_scale = HEAD_DIM ** (-0.5)
     first_col = lax.axis_index("tensor") * col_count
+
+    def compute_lines_by_axis(in_array, along_axis):
+        g_now = axis_size(along_axis)
+        tile_out, state_now, outer = (g_now, axis_index(along_axis), in_array.shape[2])
+        queue = []
+        for w in tuple(range(tile_out)):
+            queue.append((w, (w + 1) % tile_out))
+        views = []
+        for w in [*range(tile_out)]:
+            views.append((w, (w - 1) % tile_out))
+        k_now = jnp.zeros(
+            (*in_array.shape[:2], tile_out * outer, *in_array.shape[3:]), in_array.dtype
+        )
+        k_now = lax.dynamic_update_slice_in_dim(k_now, in_array, state_now * outer, axis=2)
+        inter = x_new = in_array
+        arr_next = tile_out // 2
+        for jj in tuple(range(1, arr_next + 1)):
+            inter = ppermute(inter, axis_name=along_axis, perm=queue)
+            k_now = lax.dynamic_update_slice_in_dim(
+                k_now, inter, (state_now - jj) % tile_out * outer, axis=2
+            )
+            if jj < tile_out - arr_next:
+                x_new = ppermute(x_new, axis_name=along_axis, perm=views)
+                k_now = lax.dynamic_update_slice_in_dim(
+                    k_now, x_new, (state_now + jj) % tile_out * outer, axis=2
+                )
+        return k_now
+
     full_images, full_cot = (
-        lax.all_gather(images, "tensor", axis=2, tiled=True),
+        compute_lines_by_axis(images, "tensor"),
         lax.all_gather(cotangent, "tensor", axis=2, tiled=True),
     )
     slot_ids = jnp.arange(slot_count, dtype=jnp.int32)

time: 568 us -> 586 us (1.032)
  waiting for transfers between devices: 261 us -> 281 us
  other arithmetic: 92.1 us -> 73.6 us
  starting transfers between devices: 46.3 us -> 63.7 us
    ppermute x0 -> x3, waiting for transfers between devices: none -> 54.8 us  [the longest x2 36.4 us: compute_lines_by_axis(): inter = ppermute(inter, axis_name=along_axis, perm=queue)]
    all_gather x1 -> x0, waiting for transfers between devices: 54.3 us -> none  [per_device(): lax.all_gather(images, 'tensor', axis=2, tiled=True)]
    ppermute x0 -> x3, starting transfers between devices: none -> 19.8 us  [the longest x2 17.7 us: compute_lines_by_axis(): inter = ppermute(inter, axis_name=along_axis, perm=queue)]
    psum x1, waiting for transfers between devices: 90.1 us -> 108 us  [per_device(): lax.psum(attn_part.astype(jnp.bfloat16), 'tensor').astype(jnp.float32)]
    all_gather x1, waiting for transfers between devices: 9.44 us -> 0.01 us  [per_device(): lax.all_gather(cotangent, 'tensor', axis=2, tiled=True)]
    ppermute x51, waiting for transfers between devices: 61.5 us -> 68.3 us  [swap_with(): return lax.ppermute(values, axis, [(i, i ^ stride) for i in range(size)])]
    unnamed x110 -> x122, local copies, waits for them, and re-layouts: 18.4 us -> 17.7 us
  transfers between devices with their start and end apart: 57 -> 59, of which waited for: 24 -> 26; matrix products, arithmetic and copies ran while one was open for 35% -> 27% of each run, Pallas kernels for 0% -> 0%
where the time goes in v1:
time: 586 us; the launch traced here: 577 us
  waiting for transfers between devices  281 us (48%)
  matrix products  82.1 us (14%)
  other arithmetic  73.6 us (13%)
  starting transfers between devices  63.7 us (11%)
  local copies, waits for them, and re-layouts  60.9 us (10%)
  between operations  15.6 us (3%)
    psum x1, waiting for transfers between devices, per_device(): lax.psum(attn_part.astype(jnp.bfloat16), 'tensor').astype(jnp.float32)  108 us
    ppermute x51, waiting for transfers between devices, swap_with(): return lax.ppermute(values, axis, [(i, i ^ stride) for i in range(size)])  68.3 us
    psum x1, waiting for transfers between devices, per_device(): lax.psum(hidden_part.astype(jnp.bfloat16), 'tensor').astype(jnp.float32)  49.5 us
    ppermute x51, starting transfers between devices, swap_with(): return lax.ppermute(values, axis, [(i, i ^ stride) for i in range(size)])  43.8 us
    ppermute x2, waiting for transfers between devices, compute_lines_by_axis(): inter = ppermute(inter, axis_name=along_axis, perm=queue)  36.4 us
    ppermute x1, waiting for transfers between devices, compute_lines_by_axis(): x_new = ppermute(x_new, axis_name=along_axis, perm=views)  18.4 us
    unnamed x122, local copies, waits for them, and re-layouts  17.7 us
    ppermute x2, starting transfers between devices, compute_lines_by_axis(): inter = ppermute(inter, axis_name=along_axis, perm=queue)  17.7 us
  transfers between devices with their start and end apart: 59, of which 26 were waited for; matrix products, arithmetic and copies ran while one was open for 27% of the time, Pallas kernels for 0%

profile of v1, /device:TPU:0, one launch (start us, length us, event | category | flops | bytes accessed | tf_op | source)
XLA Modules:
  0.0 576.6 jit_solution(13429548602923048205)
XLA Ops:
  13.3 18.4 %collective-permute-done = bf16[4,320,256]{2,1,0:T(8,128)(2,1)S(1)} collective-permute-done((bf16[4,320,256]{2,1,0:T(8,128)(2,1)}, bf16[4,320,256]{2,1,0:T(8,128)(2,1)S(1)}, u32[]{:S(2)}, u32[]{:S(2)}) %collective-permute-start) | collective-permute-done | bytes 655392 | tf_op jit(solution)/shard_map/ppermute | solution.py:125
  31.7 14.6 %collective-permute-start.2 = (bf16[4,320,256]{2,1,0:T(8,128)(2,1)S(1)}, bf16[4,320,256]{2,1,0:T(8,128)(2,1)}, u32[]{:S(2)}, u32[]{:S(2)}) collective-permute-start(bf16[4,320,256]{2,1,0:T(8,128)(2,1)S(1)} %collective-permute-done), channel_id=1, source_target_pairs={{0,1},{1,2},{2,3},{3,0},{4,5},{5,6},{6,7},{7,4},{8,9},{9,10},{10,1... | collective-permute-start | bytes 1966088 | tf_op jit(solution)/shard_map/ppermute | solution.py:125
  49.5 18.4 %collective-permute-done.1 = bf16[4,320,256]{2,1,0:T(8,128)(2,1)} collective-permute-done((bf16[4,320,256]{2,1,0:T(8,128)(2,1)}, bf16[4,320,256]{2,1,0:T(8,128)(2,1)}, u32[]{:S(2)}, u32[]{:S(2)}) %collective-permute-start.1) | collective-permute-done | bytes 655392 | tf_op jit(solution)/shard_map/ppermute | solution.py:130
  69.1 18.0 %collective-permute-done.2 = bf16[4,320,256]{2,1,0:T(8,128)(2,1)} collective-permute-done((bf16[4,320,256]{2,1,0:T(8,128)(2,1)S(1)}, bf16[4,320,256]{2,1,0:T(8,128)(2,1)}, u32[]{:S(2)}, u32[]{:S(2)}) %collective-permute-start.2) | collective-permute-done | bytes 655392 | tf_op jit(solution)/shard_map/ppermute | solution.py:125
  96.4 6.7 %reshape.273 = bf16[4,320,3,4,64]{4,3,2,1,0:T(4,128)(2,1)} reshape(bf16[1280,768]{1,0:T(8,128)(2,1)} %add_convert_fusion.3) | data formatting | bytes 3932160 | tf_op jit(solution)/shard_map/reshape | solution.py:151
  136.0 107.9 %all-reduce.3.cloned.1.call-done = bf16[1280,1024]{1,0:T(8,128)(2,1)} async-done(((bf16[1280,1024]{1,0:T(8,128)(2,1)}), bf16[1280,1024]{1,0:T(8,128)(2,1)}) %all-reduce.3.cloned.1.call-update) | async-done | bytes 2621456 | tf_op jit(solution)/shard_map/psum | solution.py:169
  243.9 5.0 fusion.63
  255.2 16.5 %fusion.60 = (bf16[1024]{0:T(1024)(128)(2,1)}, bf16[1280,1024]{1,0:T(8,128)(2,1)}, f32[1280,1024]{1,0:T(8,128)S(1)}) fusion(f32[1280,1024]{1,0:T(8,128)S(1)} %fusion.59, f32[1024]{0:T(1024)S(1)} %copy-done.47, bf16[1280,1024]{1,0:T(8,128)(2,1)S(1)} %get-tuple-element.44, bf16[1024,1024]{1,0:T(8,128)(2,1)S(1)} %copy-done), kind=kOutput, calls=%fused_computation.184 | convolution fusion | flops 2781346816 | bytes 17831936 | tf_op jit(solution)/shard_map/rd,fd->rf/dot_general | solution.py:181
  273.1 4.5 fusion.68
  277.6 4.5 convolution_convert_fusion.3
  282.2 6.9 %convolution_convert_fusion.2 = bf16[1280,1024]{1,0:T(8,128)(2,1)} fusion(bf16[1280,1024]{1,0:T(8,128)(2,1)} %get-tuple-element.30, bf16[1024,1024]{1,0:T(8,128)(2,1)} %param.26), kind=kOutput, calls=%fused_computation.55 | convolution fusion | flops 2685665280 | bytes 7340032 | tf_op jit(solution)/shard_map/rf,df->rd/dot_general | solution.py:186
  289.1 8.6 %fusion.58 = f32[1024,1024]{1,0:T(8,128)} fusion(bf16[1280,1024]{1,0:T(8,128)(2,1)} %get-tuple-element.30, f32[1280,1024]{1,0:T(8,128)} %copy-done.3, f32[1024]{0:T(1024)S(1)} %copy-done.54, f32[1024]{0:T(1024)S(1)} %copy-done.42, f32[1280]{0:T(1024)S(1)} %copy-done.32, f32[1280]{0:T(1024)S(1)} %copy-done.27), kind=kOutput, calls=%fused_computation.182 | convolution fusion | flops 2690908160 | bytes 12077056 | tf_op jit(solution)/shard_map/rd,rf->df/dot_general | solution.py:185
  314.2 11.5 %collective-permute-done.46 = bf16[256,1024]{1,0:T(8,128)(2,1)S(1)} collective-permute-done((bf16[256,1024]{1,0:T(8,128)(2,1)S(1)}, bf16[256,1024]{1,0:T(8,128)(2,1)S(1)}, u32[]{:S(2)}, u32[]{:S(2)}) %collective-permute-start.46) | collective-permute-done | bytes 524320 | tf_op jit(solution)/shard_map/ppermute | solution.py:41
  326.6 8.1 %collective-permute-done.37 = bf16[256,1024]{1,0:T(8,128)(2,1)S(1)} collective-permute-done((bf16[256,1024]{1,0:T(8,128)(2,1)S(1)}, bf16[256,1024]{1,0:T(8,128)(2,1)S(1)}, u32[]{:S(2)}, u32[]{:S(2)}) %collective-permute-start.37) | collective-permute-done | bytes 524320 | tf_op jit(solution)/shard_map/ppermute | solution.py:41
  337.7 6.4 %collective-permute-done.38 = bf16[128,1024]{1,0:T(8,128)(2,1)S(1)} collective-permute-done((bf16[128,1024]{1,0:T(8,128)(2,1)S(1)}, bf16[128,1024]{1,0:T(8,128)(2,1)S(1)}, u32[]{:S(2)}, u32[]{:S(2)}) %collective-permute-start.38) | collective-permute-done | bytes 262176 | tf_op jit(solution)/shard_map/ppermute | solution.py:41
  354.7 49.5 %all-reduce.5.cloned.1.call-done = bf16[1280,1024]{1,0:T(8,128)(2,1)} async-done(((bf16[1280,1024]{1,0:T(8,128)(2,1)}), bf16[1280,1024]{1,0:T(8,128)(2,1)}) %all-reduce.5.cloned.1.call-update) | async-done | bytes 2621456 | tf_op jit(solution)/shard_map/psum | solution.py:187
  406.8 5.5 multiply_reduce_fusion.1
  420.8 6.2 %fusion.29 = bf16[4,320,1,4,64]{1,4,3,0,2:T(8,128)(2,1)} fusion(bf16[4,320,4,64]{1,3,2,0:T(8,128)(2,1)S(1)} %copy.54, f32[4,4,320]{2,1,0:T(4,128)} %bitcast.109, f32[4,4,320,320]{2,3,1,0:T(8,128)} %copy-done.2, pred[4,320]{1,0:T(4,128)(4,1)S(1)} %copy-done.37), kind=kOutput, calls=%fused_computation.80 | convolution fusion | flops 216596480 | bytes 7886080 | tf_op jit(solution)/shard_map/bhqk,bqhe->bkhe/dot_general | solution.py:218
  427.0 5.4 multiply_reduce_fusion
  441.1 5.4 copy.59
  446.5 4.9 convert_element_type.555
  451.5 4.7 fusion.69
  530.4 5.3 fusion.21
  541.3 6.7 %fusion.5 = (bf16[1024]{0:T(1024)(128)(2,1)S(1)}, bf16[1280]{0:T(1024)(128)(2,1)S(1)}, bf16[1280]{0:T(1024)(128)(2,1)S(1)}, f32[1280,1024]{1,0:T(8,128)}) fusion(bf16[1280,1024]{1,0:T(8,128)(2,1)} %convolution_convert_fusion, f32[1280]{0:T(1024)S(1)} %copy-done.34, f32[1280]{0:T(1024)S(1)} %copy-done.38, f32[1280]{0:T(1024)S(1)} %reshape.271, ...), kind=kLoop, calls=%fused_computation.14 | loop fusion | flops 14414336 | bytes 10512384 | tf_op jit(solution)/shard_map/reduce_sum | solution.py:255
  (363 shorter events, 211.4 us)
Async XLA Ops:
  7.2 128.8 %all-gather.2.cloned.1.call-start = ((), (), s32[]{:S(2)}) async-start(), calls=%async_computation.3 | async-start | bytes 3276800 | tf_op jit(solution)/shard_map/all_gather | solution.py:138
  7.3 24.4 %collective-permute-start = (bf16[4,320,256]{2,1,0:T(8,128)(2,1)}, bf16[4,320,256]{2,1,0:T(8,128)(2,1)S(1)}, u32[]{:S(2)}, u32[]{:S(2)}) collective-permute-start(bf16[4,320,256]{2,1,0:T(8,128)(2,1)} %param.15), channel_id=1, source_target_pairs={{0,1},{1,2},{2,3},{3,0},{4,5},{5,6},{6,7},{7,4},{8,9},{9,10},{10,1... | collective-permute-start | bytes 1966088 | tf_op jit(solution)/shard_map/ppermute | solution.py:125
  10.4 57.5 %collective-permute-start.1 = (bf16[4,320,256]{2,1,0:T(8,128)(2,1)}, bf16[4,320,256]{2,1,0:T(8,128)(2,1)}, u32[]{:S(2)}, u32[]{:S(2)}) collective-permute-start(bf16[4,320,256]{2,1,0:T(8,128)(2,1)} %param.15), channel_id=1, source_target_pairs={{0,3},{1,0},{2,1},{3,2},{4,7},{5,4},{6,5},{7,6},{8,11},{9,8},{10,9... | collective-permute-start | bytes 1966088 | tf_op jit(solution)/shard_map/ppermute | solution.py:130
  12.5 231.5 %all-reduce.3.cloned.1.call-start = ((), (), s32[]{:S(2)}) async-start(), calls=%async_computation.2 | async-start | bytes 5242880 | tf_op jit(solution)/shard_map/psum | solution.py:169
  31.7 55.4 %collective-permute-start.2 = (bf16[4,320,256]{2,1,0:T(8,128)(2,1)S(1)}, bf16[4,320,256]{2,1,0:T(8,128)(2,1)}, u32[]{:S(2)}, u32[]{:S(2)}) collective-permute-start(bf16[4,320,256]{2,1,0:T(8,128)(2,1)S(1)} %collective-permute-done), channel_id=1, source_target_pairs={{0,1},{1,2},{2,3},{3,0},{4,5},{5,6},{6,7},{7,4},{8,9},{9,10},{10,1... | collective-permute-start | bytes 1966088 | tf_op jit(solution)/shard_map/ppermute | solution.py:125
  129.8 274.4 %all-reduce.5.cloned.1.call-start = ((), (), s32[]{:S(2)}) async-start(), calls=%async_computation.4 | async-start | bytes 5242880 | tf_op jit(solution)/shard_map/psum | solution.py:187
  300.8 200.8 %reduce-scatter.3.cloned.1.call-start = ((), (), s32[]{:S(2)}) async-start(), calls=%async_computation.5 | async-start | bytes 3276800 | tf_op jit(solution)/shard_map/reduce_scatter | solution.py:189
  307.0 28.6 %collective-permute-start.53 = (bf16[1024]{0:T(1024)(128)(2,1)S(1)}, bf16[1024]{0:T(1024)(128)(2,1)S(1)}, u32[]{:S(2)}, u32[]{:S(2)}) collective-permute-start(bf16[1024]{0:T(1024)(128)(2,1)S(1)} %add_convert_fusion.18), channel_id=1, source_target_pairs={{0,16},{4,20},{8,24},{12,28},{16,0},{20,4},{24,8},{28,12},{1,17},{... | collective-permute-start | bytes 6152 | tf_op jit(solution)/shard_map/ppermute | solution.py:41
  310.9 14.9 %collective-permute-start.46 = (bf16[256,1024]{1,0:T(8,128)(2,1)S(1)}, bf16[256,1024]{1,0:T(8,128)(2,1)S(1)}, u32[]{:S(2)}, u32[]{:S(2)}) collective-permute-start(bf16[256,1024]{1,0:T(8,128)(2,1)S(1)} %dynamic-slice_convert_fusion.3), channel_id=1, source_target_pairs={{0,8},{4,12},{8,0},{12,4},{16,24},{20,28},{24,16},{28,20},{1,9},{5... | collective-permute-start | bytes 1572872 | tf_op jit(solution)/shard_map/ppermute | solution.py:41
  313.0 21.7 %collective-permute-start.37 = (bf16[256,1024]{1,0:T(8,128)(2,1)S(1)}, bf16[256,1024]{1,0:T(8,128)(2,1)S(1)}, u32[]{:S(2)}, u32[]{:S(2)}) collective-permute-start(bf16[256,1024]{1,0:T(8,128)(2,1)S(1)} %dynamic-slice_convert_fusion.4), channel_id=1, source_target_pairs={{0,8},{4,12},{8,0},{12,4},{16,24},{20,28},{24,16},{28,20},{1,9},{5... | collective-permute-start | bytes 1572872 | tf_op jit(solution)/shard_map/ppermute | solution.py:41
  313.6 31.2 %collective-permute-start.44 = (bf16[1024]{0:T(1024)(128)(2,1)S(1)}, bf16[1024]{0:T(1024)(128)(2,1)S(1)}, u32[]{:S(2)}, u32[]{:S(2)}) collective-permute-start(bf16[1024]{0:T(1024)(128)(2,1)S(1)} %add_convert_fusion.21), channel_id=1, source_target_pairs={{0,16},{4,20},{8,24},{12,28},{16,0},{20,4},{24,8},{28,12},{1,17},{... | collective-permute-start | bytes 6152 | tf_op jit(solution)/shard_map/ppermute | solution.py:41
  336.2 13.3 %collective-permute-start.48 = (bf16[128,1024]{1,0:T(8,128)(2,1)S(1)}, bf16[128,1024]{1,0:T(8,128)(2,1)S(1)}, u32[]{:S(2)}, u32[]{:S(2)}) collective-permute-start(bf16[128,1024]{1,0:T(8,128)(2,1)S(1)} %add_convert_fusion.4), channel_id=1, source_target_pairs={{0,16},{4,20},{8,24},{12,28},{16,0},{20,4},{24,8},{28,12},{1,17},{... | collective-permute-start | bytes 786440 | tf_op jit(solution)/shard_map/ppermute | solution.py:41
  350.4 112.2 %collective-permute-start.49 = (bf16[256,1024]{1,0:T(8,128)(2,1)}, bf16[256,1024]{1,0:T(8,128)(2,1)}, u32[]{:S(2)}, u32[]{:S(2)}) collective-permute-start(bf16[256,1024]{1,0:T(8,128)(2,1)} %maximum_select_fusion.9), channel_id=1, source_target_pairs={{0,8},{4,12},{8,0},{12,4},{16,24},{20,28},{24,16},{28,20},{1,9},{5... | collective-permute-start | bytes 1572872 | tf_op jit(solution)/shard_map/ppermute | solution.py:41
  353.2 112.1 %collective-permute-start.40 = (bf16[256,1024]{1,0:T(8,128)(2,1)}, bf16[256,1024]{1,0:T(8,128)(2,1)}, u32[]{:S(2)}, u32[]{:S(2)}) collective-permute-start(bf16[256,1024]{1,0:T(8,128)(2,1)} %maximum_select_fusion.8), channel_id=1, source_target_pairs={{0,8},{4,12},{8,0},{12,4},{16,24},{20,28},{24,16},{28,20},{1,9},{5... | collective-permute-start | bytes 1572872 | tf_op jit(solution)/shard_map/ppermute | solution.py:41
  437.2 129.2 %reduce-scatter.5.cloned.1.call-start = ((), (), s32[]{:S(2)}) async-start(), calls=%async_computation.6 | async-start | bytes 3276800 | tf_op jit(solution)/shard_map/reduce_scatter | solution.py:248
  437.2 31.8 %collective-permute-start.27 = (bf16[1024]{0:T(1024)(128)(2,1)S(1)}, bf16[1024]{0:T(1024)(128)(2,1)S(1)}, u32[]{:S(2)}, u32[]{:S(2)}) collective-permute-start(bf16[1024]{0:T(1024)(128)(2,1)S(1)} %copy-done.45), channel_id=1, source_target_pairs={{0,4},{4,0},{8,12},{12,8},{16,20},{20,16},{24,28},{28,24},{1,5},{5... | collective-permute-start | bytes 6152 | tf_op jit(solution)/shard_map/ppermute | solution.py:41
  437.3 31.8 %collective-permute-start.30 = (bf16[1024]{0:T(1024)(128)(2,1)S(1)}, bf16[1024]{0:T(1024)(128)(2,1)S(1)}, u32[]{:S(2)}, u32[]{:S(2)}) collective-permute-start(bf16[1024]{0:T(1024)(128)(2,1)S(1)} %copy-done.44), channel_id=1, source_target_pairs={{0,4},{4,0},{8,12},{12,8},{16,20},{20,16},{24,28},{28,24},{1,5},{5... | collective-permute-start | bytes 6152 | tf_op jit(solution)/shard_map/ppermute | solution.py:41
  437.8 34.9 %collective-permute-start.33 = (bf16[1024]{0:T(1024)(128)(2,1)S(1)}, bf16[1024]{0:T(1024)(128)(2,1)S(1)}, u32[]{:S(2)}, u32[]{:S(2)}) collective-permute-start(bf16[1024]{0:T(1024)(128)(2,1)S(1)} %get-tuple-element.27), channel_id=1, source_target_pairs={{0,4},{4,0},{8,12},{12,8},{16,20},{20,16},{24,28},{28,24},{1,5},{5... | collective-permute-start | bytes 6152 | tf_op jit(solution)/shard_map/ppermute | solution.py:41
  462.7 18.7 %collective-permute-start.21 = (bf16[128,1024]{1,0:T(8,128)(2,1)S(1)}, bf16[128,1024]{1,0:T(8,128)(2,1)S(1)}, u32[]{:S(2)}, u32[]{:S(2)}) collective-permute-start(bf16[128,1024]{1,0:T(8,128)(2,1)S(1)} %dynamic-slice_convert_fusion.8), channel_id=1, source_target_pairs={{0,4},{4,0},{8,12},{12,8},{16,20},{20,16},{24,28},{28,24},{1,5},{5... | collective-permute-start | bytes 786440 | tf_op jit(solution)/shard_map/ppermute | solution.py:41
  468.5 21.5 %collective-permute-start.12 = (bf16[512,768]{0,1:T(8,128)(2,1)}, bf16[512,768]{0,1:T(8,128)(2,1)S(1)}, u32[]{:S(2)}, u32[]{:S(2)}) collective-permute-start(bf16[512,768]{0,1:T(8,128)(2,1)} %dynamic-slice_convert_fusion.2), channel_id=1, source_target_pairs={{0,4},{4,0},{8,12},{12,8},{16,20},{20,16},{24,28},{28,24},{1,5},{5... | collective-permute-start | bytes 2359304 | tf_op jit(solution)/shard_map/ppermute | solution.py:41
  469.0 57.0 %collective-permute-start.50 = (bf16[512,1024]{1,0:T(8,128)(2,1)S(1)}, bf16[512,1024]{1,0:T(8,128)(2,1)}, u32[]{:S(2)}, u32[]{:S(2)}) collective-permute-start(bf16[512,1024]{1,0:T(8,128)(2,1)S(1)} %maximum_select_fusion.4), channel_id=1, source_target_pairs={{0,4},{4,0},{8,12},{12,8},{16,20},{20,16},{24,28},{28,24},{1,5},{5... | collective-permute-start | bytes 3145736 | tf_op jit(solution)/shard_map/ppermute | solution.py:41
  472.7 57.7 %collective-permute-start.41 = (bf16[512,1024]{1,0:T(8,128)(2,1)}, bf16[512,1024]{1,0:T(8,128)(2,1)}, u32[]{:S(2)}, u32[]{:S(2)}) collective-permute-start(bf16[512,1024]{1,0:T(8,128)(2,1)} %maximum_select_fusion.3), channel_id=1, source_target_pairs={{0,4},{4,0},{8,12},{12,8},{16,20},{20,16},{24,28},{28,24},{1,5},{5... | collective-permute-start | bytes 3145736 | tf_op jit(solution)/shard_map/ppermute | solution.py:41
  488.5 20.9 %collective-permute-start.29 = (bf16[1024]{0:T(1024)(128)(2,1)S(1)}, bf16[1024]{0:T(1024)(128)(2,1)S(1)}, u32[]{:S(2)}, u32[]{:S(2)}) collective-permute-start(bf16[1024]{0:T(1024)(128)(2,1)S(1)} %add_convert_fusion.30), channel_id=1, source_target_pairs={{0,16},{4,20},{8,24},{12,28},{16,0},{20,4},{24,8},{28,12},{1,17},{... | collective-permute-start | bytes 6152 | tf_op jit(solution)/shard_map/ppermute | solution.py:41
  494.4 22.5 %collective-permute-start.32 = (bf16[1024]{0:T(1024)(128)(2,1)S(1)}, bf16[1024]{0:T(1024)(128)(2,1)S(1)}, u32[]{:S(2)}, u32[]{:S(2)}) collective-permute-start(bf16[1024]{0:T(1024)(128)(2,1)S(1)} %add_convert_fusion.27), channel_id=1, source_target_pairs={{0,16},{4,20},{8,24},{12,28},{16,0},{20,4},{24,8},{28,12},{1,17},{... | collective-permute-start | bytes 6152 | tf_op jit(solution)/shard_map/ppermute | solution.py:41
  (94 other events, 1224.2 us)
Sparse Core Ops, SparseCore 0:
  12.6 85.1 all-gather.1
  129.9 113.9 all-reduce.2
  301.0 103.1 all-reduce.4
  437.3 51.2 reduce-scatter.2
  504.4 49.9 reduce-scatter.4
